TPU v7x, 32 devices: a whole 2x2x4 slice. The times are simulated.
32 devices in a mesh: member: 2 (over x), wave: 16 (over z, y, core).
Axes of the slice: x: 2, y: 2, z: 4, core: 2. Of those that a mesh axis runs over, the one named last changes fastest.
Arguments:
- vorticity: bfloat16 [2560, 32, 1280], P(('member', 'wave')), parts along dimension 0, may hold values from -6 to 6
- divergence: bfloat16 [2560, 32, 1280], P(('member', 'wave')), parts along dimension 0, may hold values from -6 to 6
- legendre: bfloat16 [1280, 16, 1280], P('wave'), may hold values from -0.0068359375 to 0.0068359375
- wave_of_slot: int32 [1280], replicated, may hold values from 0 to 1279, as said below
- cycle_points: int32 [16], P('wave'), may hold values from 20 to 5136, as said below
- cos_squared: float32 [16], P('wave'), may hold values from 0.25 to 1
Outputs:
- grid: bfloat16 [32, 96, 5136], P(('member', 'wave')), parts along dimension 0
There are 2 independent parts, one for each index of `member`. A program takes and returns all parts, laid end to end along the dimension named above; an argument that names none is the same for every part. Nothing has to cross between parts.
Inputs may be any that keep to these rules, and one draw needn't show every extreme that they name: `wave_of_slot`: each wavenumber appears in exactly one slot. `cycle_points`: every count is a multiple of 4; some cycle has 5136 points.
All inputs are finite; a program needn't handle non-finite values.
Results may differ from a plain program's by a relative error of at most 0.0063.
Values may be sent and summed in bfloat16 or wider, within the bound.
A program may use at most 192 MiB of HBM per device.

v0:
```python
import functools

import jax
import jax.numpy as jnp
from jax import lax
from jax.experimental import pallas as pl
from jax.experimental.pallas import tpu as pltpu
from jax.sharding import PartitionSpec as P

NLON = 5136
LANES = 128
COS = (1.0, -1 / 2, 1 / 24, -1 / 720, 1 / 40320, -1 / 3628800, 1 / 479001600,
       -1 / 87178291200, 1 / 20922789888000, -1 / 6402373705728000)
SIN = (1.0, -1 / 6, 1 / 120, -1 / 5040, 1 / 362880, -1 / 39916800, 1 / 6227020800,
       -1 / 1307674368000, 1 / 355687428096000, -1 / 121645100408832000)


def slot_block(slots):
    return max(b for b in range(1, 17) if slots % b == 0)


def degree_coefs(wave, count):
    degree = wave + lax.broadcasted_iota(jnp.int32, (wave.shape[0], count), 1)
    living = degree < count
    positive = living & (degree > 0)
    m = wave.astype(jnp.float32)
    n = degree.astype(jnp.float32)
    inverse = jnp.where(positive, -(count / 4.0) / jnp.maximum(n * (n + 1.0), 1.0), 0.0)

    def eps(x):
        return jnp.sqrt(jnp.maximum(x * x - m * m, 0.0) / jnp.maximum(4.0 * x * x - 1.0, 1.0))

    lower = jnp.where(positive, eps(n), 0.0)
    upper = jnp.where(degree + 1 < count, eps(n + 1.0), 0.0)
    live = living.astype(jnp.float32)
    return live, inverse * m, inverse * (n + 1.0) * lower, -inverse * n * upper


def slot_fourier(values, live, along, before, after, zd):
    count = values.shape[-1]
    p = values.astype(jnp.float32)
    lon = p * along
    lat = pltpu.roll(p, 1, 1) * before + pltpu.roll(p, count - 1, 1) * after
    left = jnp.concatenate([p * live, lon, lat], axis=0).astype(jnp.bfloat16)
    sums = lax.dot_general(left, zd, (((1,), (1,)), ((), ())), preferred_element_type=jnp.float32)
    rows = p.shape[0]
    lev = zd.shape[0] // 4
    plain, a, b = sums[:rows], sums[rows : 2 * rows], sums[2 * rows :]
    zr, zi, dr, di = (slice(g * lev, (g + 1) * lev) for g in range(4))
    turned = jnp.concatenate([-a[:, di], a[:, dr], -a[:, zi], a[:, zr]], axis=1)
    lane = lax.broadcasted_iota(jnp.int32, b.shape, 1)
    winds = turned + jnp.where(lane < 2 * lev, -b, b)
    return jnp.concatenate([winds, plain], axis=1)


def horner(coefs, x):
    total = jnp.full_like(x, coefs[-1])
    for c in coefs[-2::-1]:
        total = total * x + c
    return total


def turn(steps, points, per_point):
    turns = jnp.round(steps * per_point)
    theta = (steps - turns * points) * (per_point * (2.0 * jnp.pi))
    square = theta * theta
    return horner(COS, square), theta * horner(SIN, square)


def basis_columns(row, points):
    slots = row.shape[1]
    column = lambda x: jnp.broadcast_to(x, (LANES, slots)).T
    step = turn(row * float(LANES), points, 1.0 / points)
    return column(row), column(step[0]), column(step[1])


def fill_basis(columns, points, basis, first, last):
    wave, step_c, step_s = columns
    slots = wave.shape[0]
    lane = lax.broadcasted_iota(jnp.int32, (16, LANES), 1).astype(jnp.float32)
    for start in range(first, last, 16):
        rows = slice(start, start + 16)
        c, s = turn(wave[rows] * lane, points, 1.0 / points)
        cs, ss = step_c[rows], step_s[rows]
        for t in range(basis.shape[1] // LANES):
            at = slice(t * LANES, (t + 1) * LANES)
            basis[rows, at] = c.astype(basis.dtype)
            basis[slots + start : slots + start + 16, at] = s.astype(basis.dtype)
            c, s = c * cs - s * ss, s * cs + c * ss


def fill_fields(arrived, wave, points, cosine_sq, count, packed):
    x = arrived.astype(jnp.float32).T
    lev = x.shape[0] // 8
    ur, ui, vr, vi, zr, zi, dr, di = (x[g * lev : (g + 1) * lev] for g in range(8))
    slots = wave.shape[1]
    m = wave.astype(jnp.float32)
    q = m * (4.0 / count)
    over = 1.0 / jnp.full_like(m, cosine_sq)
    ulr, uli, vlr, vli = -q * ui, q * ur, -q * vi, q * vr
    fields = (
        (ur, ui), (vr, vi), (ulr, uli), (vlr, vli),
        (vlr * over - zr, vli * over - zi), (dr - ulr * over, di - uli * over),
    )
    weight = jnp.where(2 * wave < points, jnp.where(wave == 0, 1.0, 2.0), 0.0)
    for f, (re, im) in enumerate(fields):
        a, b = re * weight, -im * weight
        for j in range(4):
            phase = (wave * j) & 3
            c = jnp.where(phase == 0, 1.0, jnp.where(phase == 2, -1.0, 0.0))
            s = jnp.where(phase == 1, 1.0, jnp.where(phase == 3, -1.0, 0.0))
            start = (j * len(fields) + f) * lev
            rows = slice(start, start + lev)
            packed[rows, :slots] = (a * c + b * s).astype(packed.dtype)
            packed[rows, slots:] = (b * c - a * s).astype(packed.dtype)


def place(quarters, points, line):
    rows = quarters.shape[0] // 4
    tiles = quarters.shape[1] // LANES
    quarter = points // 4
    lane = lax.broadcasted_iota(jnp.int32, (rows, LANES), 1)
    line[...] = jnp.zeros_like(line)
    for j in range(4):
        offset = quarter * j
        base = pl.multiple_of(offset // LANES * LANES, LANES)
        shift = offset - base
        previous = jnp.zeros((rows, LANES), jnp.float32)
        for t in range(tiles + 1):
            rolled = jnp.zeros((rows, LANES), jnp.float32)
            if t < tiles:
                tile = quarters[j * rows : (j + 1) * rows, t * LANES : (t + 1) * LANES]
                tile = jnp.where(lane + t * LANES < quarter, tile.astype(jnp.float32), 0.0)
                rolled = pltpu.roll(tile, shift, 1)
            moved = jnp.where(lane < shift, previous, rolled).astype(line.dtype)
            at = pl.ds(pl.multiple_of(base + t * LANES, LANES), LANES)
            line[:, at] = line[:, at] + moved
            previous = rolled


def send_groups(blocks):
    return [(0, (blocks + 1) // 2), ((blocks + 1) // 2, blocks)]


def exchange_kernel(
    groups,     points_ref, cosine_ref, slots_ref, wave_ref, zeta_ref, delta_ref, values_ref, quarters_ref,
    sums, sent, held, basis, packed, send_sem, recv_sem,
):
    step = pl.program_id(0)
    cycles, devices, blocks, sb, columns = held.shape
    count = zeta_ref.shape[-1]
    me = lax.axis_index("wave")
    barrier = pltpu.get_barrier_semaphore()

    def copy(group, off, cycle):
        start, stop = groups[group]
        to = lax.rem(me + off, devices)
        return pltpu.make_async_remote_copy(
            src_ref=sent.at[to * cycles + cycle, start:stop],
            dst_ref=held.at[cycle, me, start:stop],
            send_sem=send_sem.at[group, cycle, off - 1],
            recv_sem=recv_sem.at[group, cycle, off - 1],
            device_id={"wave": to},
            device_id_type=pl.DeviceIdType.MESH,
        )

    def each(group, act):
        for cycle in range(cycles):
            pl.loop(1, devices)(lambda off: act(copy(group, off, cycle)))

    def send(group):
        if group == 0:
            pl.semaphore_wait(barrier, devices - 1)
        each(group, lambda c: c.start())

    @pl.when(step == 0)
    def _():
        @pl.loop(1, devices)
        def _(off):
            pl.semaphore_signal(
                barrier, inc=1, device_id={"wave": lax.rem(me + off, devices)},
                device_id_type=pl.DeviceIdType.MESH,
            )

    for group, (_, stop) in enumerate(groups[:-1]):
        pl.when(step == stop)(functools.partial(send, group))

    first = me * (blocks * sb) + step * sb
    row = lax.broadcasted_iota(jnp.int32, (sb, 1), 0)
    waves = jnp.zeros((sb, 1), jnp.int32)
    for s in range(sb):
        waves = jnp.where(row == s, slots_ref[first + s], waves)
    coefs = degree_coefs(waves, count)
    rows = values_ref.shape[1]
    for s in range(sb):
        zd = jnp.concatenate([zeta_ref[s], delta_ref[s]], axis=0)
        out = slot_fourier(values_ref[s], *(c[s : s + 1] for c in coefs), zd)
        sums[pl.ds(s, rows, sb), :] = out
    sent[:, step] = sums[...].astype(sent.dtype).reshape(rows, sb, columns)

    @pl.when(step == blocks - 1)
    def _():
        wave = wave_ref[...].reshape(1, -1)
        slots = wave.shape[1]
        for cycle in range(cycles):
            points = points_ref[cycle]
            points_f = jnp.full((1, 1), points, jnp.int32).astype(jnp.float32)
            cols = basis_columns(wave.astype(jnp.float32), points_f)
            early = slots // 4 // 16 * 16
            fill_basis(cols, points_f, basis, 0, early)
            if cycle == 0:
                send(len(groups) - 1)
            fill_basis(cols, points_f, basis, early, slots)
            if cycle == 0:
                for c in range(cycles):
                    held[c, me] = sent[me * cycles + c]
                for group in range(len(groups)):
                    each(group, lambda c: c.wait_recv())
            arrived = held[cycle].reshape(slots, columns)
            fill_fields(arrived, wave, points, cosine_ref[cycle], count, packed)
            width = basis.shape[1]
            for start in range(0, width, 256):
                at = slice(start, min(start + 256, width))
                quarters_ref[cycle, :, at] = jnp.dot(
                    packed[...], basis[:, at], preferred_element_type=jnp.float32
                ).astype(quarters_ref.dtype)
        for group in range(len(groups)):
            each(group, lambda c: c.wait_send())


def cycle_quarters(points, cosine_sq, wave_of_slot, vorticity, divergence, legendre):
    slots, half, count = vorticity.shape
    lines = legendre.shape[1]
    cycles = points.shape[0]
    devices = lines // cycles
    columns = 4 * half
    rows = 6 * half
    width = -(-NLON // 4 // LANES) * LANES
    sb = slot_block(slots)
    blocks = slots // sb
    block = lambda n: pl.BlockSpec((sb, n, count), lambda i: (i, 0, 0))
    smem = pl.BlockSpec(memory_space=pltpu.SMEM)
    groups = send_groups(blocks)
    sem = pltpu.SemaphoreType.DMA((len(groups), cycles, devices - 1))
    return pl.pallas_call(
        functools.partial(exchange_kernel, groups),
        grid=(blocks,),
        in_specs=[
            smem, smem, smem, pl.BlockSpec(memory_space=pltpu.VMEM),
            block(half), block(half), block(lines),
        ],
        out_specs=pl.BlockSpec((cycles, 2 * rows, width), lambda i: (0, 0, 0)),
        out_shape=jax.ShapeDtypeStruct((cycles, 2 * rows, width), jnp.bfloat16),
        scratch_shapes=[
            pltpu.VMEM((lines * sb, columns), jnp.float32),
            pltpu.VMEM((lines, blocks, sb, columns), jnp.bfloat16),
            pltpu.VMEM((cycles, devices, blocks, sb, columns), jnp.bfloat16),
            pltpu.VMEM((2 * devices * slots, width), jnp.bfloat16),
            pltpu.VMEM((2 * rows, 2 * devices * slots), jnp.bfloat16),
            sem,
            sem,
        ],
        compiler_params=pltpu.CompilerParams(collective_id=0, has_side_effects=True),
    )(points, cosine_sq, wave_of_slot, wave_of_slot, vorticity, divergence, legendre)


def place_kernel(points_ref, quarters_ref, out_ref, line):
    place(quarters_ref.at[0], points_ref[pl.program_id(0)], line)
    out_ref[0] = line[:, : out_ref.shape[2]]


def placed(quarters, points):
    cycles, rows, width = quarters.shape
    rows = rows // 4
    return pl.pallas_call(
        place_kernel,
        grid=(cycles,),
        in_specs=[
            pl.BlockSpec(memory_space=pltpu.SMEM),
            pl.BlockSpec((1, 4 * rows, width), lambda i: (i, 0, 0)),
        ],
        out_specs=pl.BlockSpec((1, rows, NLON), lambda i: (i, 0, 0)),
        out_shape=jax.ShapeDtypeStruct((cycles, rows, NLON), jnp.bfloat16),
        scratch_shapes=[pltpu.VMEM((rows, 4 * width + 2 * LANES), jnp.bfloat16)],
    )(points, quarters)


def body(vorticity, divergence, legendre, wave_of_slot, cycle_points, cos_squared):
    quarters = cycle_quarters(
        cycle_points, cos_squared, wave_of_slot, vorticity, divergence, legendre
    )
    return placed(quarters, cycle_points)


def solution(mesh):
    return jax.shard_map(
        body,
        mesh=mesh,
        in_specs=(
            P(("member", "wave"), None, None),
            P(("member", "wave"), None, None),
            P("wave", None, None),
            P(),
            P("wave"),
            P("wave"),
        ),
        out_specs=P(("member", "wave"), None, None),
        check_vma=False,
    )
```

profile of v0, /device:TPU:0, one launch (start us, length us, event | category | flops | bytes accessed | tf_op | source)
XLA Modules:
  0.0 28.1 jit_solution(8761987845443450914)
XLA Ops:
  1.3 24.0 %shard_map.64.quarters_ref = bf16[1,384,1408]{2,1,0:T(8,128)(2,1)} custom-call(s32[1]{0:T(128)S(6)} %copy.7.points_ref, f32[1]{0:T(128)S(6)} %copy.8.cosine_ref, s32[1280]{0:T(1024)} %wave_ref.1, s32[1280]{0:T(1024)} %wave_ref.1, bf16[80,32,1280]{2,1,0:T(8,128)(2,1)} %zeta_ref.1, bf16[80,32,1280]{2,1,0:T(8,128)(2,1)} %delta_ref.1, ...), custom_call_target="tpu_custom_call" | custom-call | tf_op jit(solution)/shard_map/pallas_call | solution.py:245
  25.3 2.8 %shard_map.65 = bf16[1,96,5136]{2,1,0:T(8,128)(2,1)} custom-call(s32[1]{0:T(128)S(6)} %copy.7.points_ref, bf16[1,384,1408]{2,1,0:T(8,128)(2,1)} %shard_map.64.quarters_ref), custom_call_target="tpu_custom_call" | custom-call | tf_op jit(solution)/shard_map/pallas_call | solution.py:275
where the time goes:
time: 28.3 us; the launch traced here: 28.1 us
  Pallas kernels  26.8 us (95%)
  between operations  1.31 us (5%)
    pallas_call x1, Pallas kernels, cycle_quarters(): pl.pallas_call(functools.partial(exchange_kernel, groups), grid=(blocks,)...  24 us
    pallas_call x1, Pallas kernels, placed(): pl.pallas_call(place_kernel, grid=(cycles,), in_specs=[pl.BlockSpec(memor...  2.82 us

commit v1 on v0

v1 whole, which is shorter than its diff:
```python
import functools

import jax
import jax.numpy as jnp
from jax import lax
from jax.experimental import pallas as pl
from jax.experimental.pallas import tpu as pltpu
from jax.sharding import PartitionSpec as P

NLON = 5136
LANES = 128
COS = (1.0, -1 / 2, 1 / 24, -1 / 720, 1 / 40320, -1 / 3628800, 1 / 479001600,
       -1 / 87178291200, 1 / 20922789888000, -1 / 6402373705728000)
SIN = (1.0, -1 / 6, 1 / 120, -1 / 5040, 1 / 362880, -1 / 39916800, 1 / 6227020800,
       -1 / 1307674368000, 1 / 355687428096000, -1 / 121645100408832000)


def slot_block(slots):
    return max(b for b in range(1, 17) if slots % b == 0)


def degree_coefs(wave, count):
    column = lax.broadcasted_iota(jnp.int32, (wave.shape[0], count), 1)
    degree = wave + column
    living = degree < count
    positive = living & (degree > 0)
    m = wave.astype(jnp.float32)
    n = degree.astype(jnp.float32)
    radius = count / 4.0
    square = n * n
    ratio = jnp.maximum(square - m * m, 0.0) / jnp.maximum(square * (4.0 * square - 1.0), 1.0)
    lower = radius * jnp.sqrt(ratio)
    upper = pltpu.roll(lower, count - 1, 1)
    along = jnp.where(positive, -radius * m / jnp.maximum(n * (n + 1.0), 1.0), 0.0)
    before = jnp.where(positive, -lower, 0.0)
    after = jnp.where((degree > 0) & (degree + 1 < count), upper, 0.0)
    return living.astype(jnp.float32), along, before, after


def slot_fourier(values, live, along, before, after, zd):
    count = values.shape[-1]
    p = values.astype(jnp.float32)
    lon = p * along
    lat = pltpu.roll(p, 1, 1) * before + pltpu.roll(p, count - 1, 1) * after
    left = jnp.concatenate([p * live, lon, lat], axis=0).astype(jnp.bfloat16)
    sums = lax.dot_general(left, zd, (((1,), (1,)), ((), ())), preferred_element_type=jnp.float32)
    rows = p.shape[0]
    lev = zd.shape[0] // 4
    plain, a, b = sums[:rows], sums[rows : 2 * rows], sums[2 * rows :]
    zr, zi, dr, di = (slice(g * lev, (g + 1) * lev) for g in range(4))
    turned = jnp.concatenate([-a[:, di], a[:, dr], -a[:, zi], a[:, zr]], axis=1)
    lane = lax.broadcasted_iota(jnp.int32, b.shape, 1)
    winds = turned + jnp.where(lane < 2 * lev, -b, b)
    return jnp.concatenate([winds, plain], axis=1)


def horner(coefs, x):
    total = jnp.full_like(x, coefs[-1])
    for c in coefs[-2::-1]:
        total = total * x + c
    return total


def turn(steps, points, per_point):
    turns = jnp.round(steps * per_point)
    theta = (steps - turns * points) * (per_point * (2.0 * jnp.pi))
    square = theta * theta
    return horner(COS, square), theta * horner(SIN, square)


def columns_of(row):
    return jnp.broadcast_to(row, (LANES, row.shape[1])).T


def fill_basis(wave_col, steps, points, basis):
    step_c, step_s = (columns_of(x) for x in steps)
    slots = wave_col.shape[0]
    lane = lax.broadcasted_iota(jnp.int32, (16, LANES), 1).astype(jnp.float32)
    for start in range(0, slots, 16):
        rows = slice(start, start + 16)
        c, s = turn(wave_col[rows] * lane, points, 1.0 / points)
        cs, ss = step_c[rows], step_s[rows]
        for t in range(basis.shape[1] // LANES):
            at = slice(t * LANES, (t + 1) * LANES)
            basis[rows, at] = c.astype(basis.dtype)
            basis[slots + start : slots + start + 16, at] = s.astype(basis.dtype)
            c, s = c * cs - s * ss, s * cs + c * ss


def fill_fields(arrived, wave, points, cosine_sq, count, packed):
    x = arrived.astype(jnp.float32).T
    lev = x.shape[0] // 8
    ur, ui, vr, vi, zr, zi, dr, di = (x[g * lev : (g + 1) * lev] for g in range(8))
    slots = wave.shape[1]
    m = wave.astype(jnp.float32)
    q = m * (4.0 / count)
    over = 1.0 / jnp.full_like(m, cosine_sq)
    ulr, uli, vlr, vli = -q * ui, q * ur, -q * vi, q * vr
    fields = (
        (ur, ui), (vr, vi), (ulr, uli), (vlr, vli),
        (vlr * over - zr, vli * over - zi), (dr - ulr * over, di - uli * over),
    )
    weight = jnp.where(2 * wave < points, jnp.where(wave == 0, 1.0, 2.0), 0.0)
    parity = jnp.where((wave & 1) == 0, 1.0, -1.0)
    half = len(fields) * lev
    for f, (re, im) in enumerate(fields):
        for part, x in enumerate((re * weight, -im * weight)):
            packed[part, f * lev : (f + 1) * lev] = x.astype(packed.dtype)
            packed[part, half + f * lev : half + (f + 1) * lev] = (x * parity).astype(packed.dtype)


def send_groups(blocks):
    return [(b, b + 1) for b in range(blocks)]


def partners(me, devices):
    if devices % 2:
        return [lax.rem(me + off, devices) for off in range(1, devices)]
    half = devices // 2
    side = me // half
    far = [(1 - side) * half + lax.rem(me + off, half) for off in range(half)]
    near = [side * half + lax.rem(me + off, half) for off in range(1, half)]
    return far + near


def exchange_kernel(
    groups, points_ref, cosine_ref, wave_hbm, zeta_hbm, delta_hbm, values_hbm, quarters_ref,
    wave_ref, wave_col, zeta_ref, delta_ref, values_ref, sums, sent, held, basis, packed,
    wave_sem, in_sem, send_sem, recv_sem,
):
    cycles, devices, blocks, sb, columns = held.shape
    count = zeta_ref.shape[-1]
    rows = values_ref.shape[1]
    me = lax.axis_index("wave")
    barrier = pltpu.get_barrier_semaphore()
    peers = partners(me, devices)

    def fetch(step):
        at = pl.ds(step * sb, sb)
        return [
            pltpu.make_async_copy(source.at[at], target.at[at], in_sem.at[k, step])
            for k, (source, target) in enumerate(
                ((zeta_hbm, zeta_ref), (delta_hbm, delta_ref), (values_hbm, values_ref))
            )
        ]

    load_wave = pltpu.make_async_copy(wave_hbm, wave_ref, wave_sem)
    load_wave.start()
    for step in range(blocks):
        for copy in fetch(step):
            copy.start()
    for to in peers:
        pl.semaphore_signal(
            barrier, inc=1, device_id={"wave": to}, device_id_type=pl.DeviceIdType.MESH
        )

    def send(group):
        start, stop = groups[group]
        for to in peers:
            for cycle in range(cycles):
                pltpu.make_async_remote_copy(
                    src_ref=sent.at[to * cycles + cycle, start:stop],
                    dst_ref=held.at[cycle, me, start:stop],
                    send_sem=send_sem.at[cycle],
                    recv_sem=recv_sem.at[cycle],
                    device_id={"wave": to},
                    device_id_type=pl.DeviceIdType.MESH,
                ).start()

    load_wave.wait()
    wave = wave_ref[...].reshape(1, -1)
    slots = wave.shape[1]
    wave_f = wave.astype(jnp.float32)
    wave_col[...] = columns_of(wave_f)

    def legendre(step, carry):
        for copy in fetch(step):
            copy.wait()
        waves = wave_col[pl.ds(me * (blocks * sb) + step * sb, sb), 0:1].astype(jnp.int32)
        coefs = degree_coefs(waves, count)
        for s in range(sb):
            slot = step * sb + s
            zd = jnp.concatenate([zeta_ref[slot], delta_ref[slot]], axis=0)
            out = slot_fourier(values_ref[slot], *(c[s : s + 1] for c in coefs), zd)
            sums[pl.ds(s, rows, sb), :] = out
        sent[:, step] = sums[...].astype(sent.dtype).reshape(rows, sb, columns)
        for cycle in range(cycles):
            mine = sums[pl.ds((me * cycles + cycle) * sb, sb), :]
            held[cycle, me, step] = mine.astype(held.dtype)
        for group, (_, stop) in enumerate(groups):
            @pl.when(step == stop - 1)
            def _():
                if group == 0:
                    pl.semaphore_wait(barrier, devices - 1)
                send(group)
        return carry

    lax.fori_loop(0, blocks, legendre, 0)
    for cycle in range(cycles):
        points = points_ref[cycle]
        points_f = jnp.full((1, 1), points, jnp.int32).astype(jnp.float32)
        steps = turn(wave_f * float(LANES), points_f, 1.0 / points_f)
        fill_basis(wave_col, steps, points_f, basis)
        others = held.at[cycle, 0 : devices - 1]
        if cycle == 0:
            for c in range(cycles):
                all_of = held.at[c, 0 : devices - 1]
                pltpu.make_async_copy(all_of, all_of, recv_sem.at[c]).wait()
        arrived = held[cycle].reshape(slots, columns)
        fill_fields(arrived, wave, points, cosine_ref[cycle], count, packed)
        width = basis.shape[1]
        half = packed.shape[1] // 2
        for start in range(0, width, 256):
            at = slice(start, min(start + 256, width))
            cosine, sine = (
                jnp.dot(
                    packed[part], basis[part * slots : (part + 1) * slots, at],
                    preferred_element_type=jnp.float32,
                )
                for part in range(2)
            )
            parts = (
                cosine[:half] + sine[:half], cosine[half:] - sine[half:],
                cosine[half:] + sine[half:], cosine[:half] - sine[:half],
            )
            for j, x in enumerate(parts):
                quarters_ref[cycle, j * half : (j + 1) * half, at] = x.astype(quarters_ref.dtype)
        pltpu.make_async_copy(others, others, send_sem.at[cycle]).wait()


def basis_width():
    return -(-(NLON // 4 + 1) // LANES) * LANES


def cycle_quarters(points, cosine_sq, wave_of_slot, vorticity, divergence, legendre):
    slots, half, count = vorticity.shape
    lines = legendre.shape[1]
    cycles = points.shape[0]
    devices = lines // cycles
    columns = 4 * half
    rows = 6 * half
    width = basis_width()
    sb = slot_block(slots)
    blocks = slots // sb
    smem = pl.BlockSpec(memory_space=pltpu.SMEM)
    hbm = pl.BlockSpec(memory_space=pltpu.HBM)
    sem = pltpu.SemaphoreType.DMA((cycles,))
    return pl.pallas_call(
        functools.partial(exchange_kernel, send_groups(blocks)),
        in_specs=[smem, smem, hbm, hbm, hbm, hbm],
        out_specs=pl.BlockSpec(memory_space=pltpu.VMEM),
        out_shape=jax.ShapeDtypeStruct((cycles, 2 * rows, width), jnp.bfloat16),
        scratch_shapes=[
            pltpu.VMEM(wave_of_slot.shape, jnp.int32),
            pltpu.VMEM((devices * slots, LANES), jnp.float32),
            pltpu.VMEM(vorticity.shape, vorticity.dtype),
            pltpu.VMEM(divergence.shape, divergence.dtype),
            pltpu.VMEM(legendre.shape, legendre.dtype),
            pltpu.VMEM((lines * sb, columns), jnp.float32),
            pltpu.VMEM((lines, blocks, sb, columns), jnp.bfloat16),
            pltpu.VMEM((cycles, devices, blocks, sb, columns), jnp.bfloat16),
            pltpu.VMEM((2 * devices * slots, width), jnp.bfloat16),
            pltpu.VMEM((2, rows, devices * slots), jnp.bfloat16),
            pltpu.SemaphoreType.DMA,
            pltpu.SemaphoreType.DMA((3, blocks)),
            sem,
            sem,
        ],
        compiler_params=pltpu.CompilerParams(
            collective_id=0, has_side_effects=True, vmem_limit_bytes=40 << 20
        ),
    )(points, cosine_sq, wave_of_slot, vorticity, divergence, legendre)


def place(quarters, points, line):
    rows = quarters.shape[0] // 4
    width = quarters.shape[1]
    tiles = width // LANES
    quarter = points // 4
    lane = lax.broadcasted_iota(jnp.int32, (rows, LANES), 1)
    line[...] = jnp.zeros_like(line)
    for j in range(4):
        turned = j % 2
        offset = quarter * (j + 1) - (width - 1) if turned else quarter * j
        offset = offset + front_lanes(width)
        base = pl.multiple_of(offset // LANES * LANES, LANES)
        shift = offset - base
        source = lane - shift if not turned else shift - 1 - lane
        source = source & (LANES - 1)
        previous = jnp.zeros((rows, LANES), jnp.float32)
        for t in range(tiles + 1):
            rolled = jnp.zeros((rows, LANES), jnp.float32)
            if t < tiles:
                u = tiles - 1 - t if turned else t
                tile = quarters[j * rows : (j + 1) * rows, u * LANES : (u + 1) * LANES]
                point = lane + u * LANES
                keep = (point > 0) & (point <= quarter) if turned else point < quarter
                tile = jnp.where(keep, tile.astype(jnp.float32), 0.0)
                rolled = jnp.take_along_axis(tile, source, axis=1)
            moved = jnp.where(lane < shift, previous, rolled).astype(line.dtype)
            at = pl.ds(pl.multiple_of(base + t * LANES, LANES), LANES)
            line[:, at] = line[:, at] + moved
            previous = rolled


def front_lanes(width):
    return width + LANES


def place_kernel(points_ref, quarters_ref, out_ref, line):
    place(quarters_ref.at[0], points_ref[pl.program_id(0)], line)
    front = front_lanes(quarters_ref.shape[2])
    out_ref[0] = line[:, front : front + out_ref.shape[2]]


def placed(quarters, points):
    cycles, rows, width = quarters.shape
    rows = rows // 4
    line = front_lanes(width) + 4 * width + 2 * LANES
    return pl.pallas_call(
        place_kernel,
        grid=(cycles,),
        in_specs=[
            pl.BlockSpec(memory_space=pltpu.SMEM),
            pl.BlockSpec((1, 4 * rows, width), lambda i: (i, 0, 0)),
        ],
        out_specs=pl.BlockSpec((1, rows, NLON), lambda i: (i, 0, 0)),
        out_shape=jax.ShapeDtypeStruct((cycles, rows, NLON), jnp.bfloat16),
        scratch_shapes=[pltpu.VMEM((rows, line), jnp.bfloat16)],
        compiler_params=pltpu.CompilerParams(vmem_limit_bytes=16 << 20),
    )(points, quarters)


def body(vorticity, divergence, legendre, wave_of_slot, cycle_points, cos_squared):
    quarters = cycle_quarters(
        cycle_points, cos_squared, wave_of_slot, vorticity, divergence, legendre
    )
    return placed(quarters, cycle_points)


def solution(mesh):
    return jax.shard_map(
        body,
        mesh=mesh,
        in_specs=(
            P(("member", "wave"), None, None),
            P(("member", "wave"), None, None),
            P("wave", None, None),
            P(),
            P("wave"),
            P("wave"),
        ),
        out_specs=P(("member", "wave"), None, None),
        check_vma=False,
    )
```

time: 28.3 us -> 27 us (0.954)
  Pallas kernels: 26.8 us -> 19.9 us
  local copies, waits for them, and re-layouts: 0 us -> 5.47 us
    pallas_call x1, Pallas kernels: 24 us -> 18.3 us  [cycle_quarters(): pl.pallas_call(functools.partial(exchange_kernel, send_groups(blocks)), i...]
    unnamed x0 -> x6, local copies, waits for them, and re-layouts: none -> 5.47 us
    pallas_call x1, Pallas kernels: 2.82 us -> 1.63 us  [placed(): pl.pallas_call(place_kernel, grid=(cycles,), in_specs=[pl.BlockSpec(memor...]
where the time goes in v1:
time: 27 us; the launch traced here: 26.7 us
  Pallas kernels  19.9 us (74%)
  local copies, waits for them, and re-layouts  5.47 us (20%)
  between operations  1.32 us (5%)
    pallas_call x1, Pallas kernels, cycle_quarters(): pl.pallas_call(functools.partial(exchange_kernel, send_groups(blocks)), i...  18.3 us
    unnamed x6, local copies, waits for them, and re-layouts  5.47 us
    pallas_call x1, Pallas kernels, placed(): pl.pallas_call(place_kernel, grid=(cycles,), in_specs=[pl.BlockSpec(memor...  1.63 us

profile of v1, /device:TPU:0, one launch (start us, length us, event | category | flops | bytes accessed | tf_op | source)
XLA Modules:
  0.0 26.7 jit_solution(17089646670475648811)
XLA Ops:
  1.3 0.0 copy-start
  1.3 2.9 %copy-done = bf16[80,32,1280]{2,1,0:T(8,128)(2,1)S(1)} copy-done((bf16[80,32,1280]{2,1,0:T(8,128)(2,1)S(1)}, bf16[80,32,1280]{2,1,0:T(8,128)(2,1)}, u32[]{:S(2)}) %copy-start) | copy-done | bytes 6553624
  4.2 0.0 copy-start.1
  4.2 1.9 %copy-done.1 = bf16[80,16,1280]{2,1,0:T(8,128)(2,1)S(1)} copy-done((bf16[80,16,1280]{2,1,0:T(8,128)(2,1)S(1)}, bf16[80,16,1280]{2,1,0:T(8,128)(2,1)}, u32[]{:S(2)}) %copy-start.1) | copy-done | bytes 3276824
  6.1 0.0 copy-start.2
  6.1 0.7 %copy-done.2 = s32[1280]{0:T(1024)S(1)} copy-done((s32[1280]{0:T(1024)S(1)}, s32[1280]{0:T(1024)}, u32[]{:S(2)}) %copy-start.2) | copy-done | bytes 5144
  6.8 18.3 %shard_map.64.quarters_ref = bf16[1,384,1408]{2,1,0:T(8,128)(2,1)S(1)} custom-call(s32[1]{0:T(128)S(6)} %copy.7.points_ref, f32[1]{0:T(128)S(6)} %copy.8.cosine_ref, s32[1280]{0:T(1024)S(1)} %copy-done.2, bf16[80,32,1280]{2,1,0:T(8,128)(2,1)S(1)} %copy-done, bf16[80,32,1280]{2,1,0:T(8,128)(2,1)} %delta_hbm.1, bf16[80,16,1280]{2,1,0:T(8,128)(2,1)S(1)} %copy-done.1), custom_call_target="tpu_custom_call" | custom-call | tf_op jit(solution)/shard_map/pallas_call | solution.py:248
  25.1 1.6 %shard_map.65 = bf16[1,96,5136]{2,1,0:T(8,128)(2,1)} custom-call(s32[1]{0:T(128)S(6)} %copy.7.points_ref, bf16[1,384,1408]{2,1,0:T(8,128)(2,1)S(1)} %shard_map.64.quarters_ref), custom_call_target="tpu_custom_call" | custom-call | tf_op jit(solution)/shard_map/pallas_call | solution.py:320
Async XLA Ops:
  1.3 2.9 %copy-start = (bf16[80,32,1280]{2,1,0:T(8,128)(2,1)S(1)}, bf16[80,32,1280]{2,1,0:T(8,128)(2,1)}, u32[]{:S(2)}) copy-start(bf16[80,32,1280]{2,1,0:T(8,128)(2,1)} %zeta_hbm.1) | copy-start | bytes 19660804
  4.2 1.9 %copy-start.1 = (bf16[80,16,1280]{2,1,0:T(8,128)(2,1)S(1)}, bf16[80,16,1280]{2,1,0:T(8,128)(2,1)}, u32[]{:S(2)}) copy-start(bf16[80,16,1280]{2,1,0:T(8,128)(2,1)} %values_hbm.1) | copy-start | bytes 9830404
  6.1 0.7 %copy-start.2 = (s32[1280]{0:T(1024)S(1)}, s32[1280]{0:T(1024)}, u32[]{:S(2)}) copy-start(s32[1280]{0:T(1024)} %wave_hbm.1) | copy-start | bytes 15364

commit v2 on v1

--- a/solution.py
+++ b/solution.py
@@ -146,9 +146,11 @@
 
     load_wave = pltpu.make_async_copy(wave_hbm, wave_ref, wave_sem)
     load_wave.start()
-    for step in range(blocks):
+    def start(step):
         for copy in fetch(step):
             copy.start()
+
+    start(0)
     for to in peers:
         pl.semaphore_signal(
             barrier, inc=1, device_id={"wave": to}, device_id_type=pl.DeviceIdType.MESH
@@ -168,6 +170,8 @@
                 ).start()
 
     load_wave.wait()
+    if blocks > 1:
+        start(1)
     wave = wave_ref[...].reshape(1, -1)
     slots = wave.shape[1]
     wave_f = wave.astype(jnp.float32)
@@ -176,6 +180,7 @@
     def legendre(step, carry):
         for copy in fetch(step):
             copy.wait()
+        pl.when(step + 2 < blocks)(lambda: start(step + 2))
         waves = wave_col[pl.ds(me * (blocks * sb) + step * sb, sb), 0:1].astype(jnp.int32)
         coefs = degree_coefs(waves, count)
         for s in range(sb):
@@ -247,7 +252,7 @@
     sem = pltpu.SemaphoreType.DMA((cycles,))
     return pl.pallas_call(
         functools.partial(exchange_kernel, send_groups(blocks)),
-        in_specs=[smem, smem, hbm, hbm, hbm, hbm],
+        in_specs=[smem] * 2 + [hbm] * 4,
         out_specs=pl.BlockSpec(memory_space=pltpu.VMEM),
         out_shape=jax.ShapeDtypeStruct((cycles, 2 * rows, width), jnp.bfloat16),
         scratch_shapes=[
@@ -269,7 +274,10 @@
         compiler_params=pltpu.CompilerParams(
             collective_id=0, has_side_effects=True, vmem_limit_bytes=40 << 20
         ),
-    )(points, cosine_sq, wave_of_slot, vorticity, divergence, legendre)
+    )(points, cosine_sq, *(
+        pltpu.with_memory_space_constraint(x, pltpu.HBM)
+        for x in (wave_of_slot, vorticity, divergence, legendre)
+    ))
 
 
 def place(quarters, points, line):
@@ -278,7 +286,6 @@
     tiles = width // LANES
     quarter = points // 4
     lane = lax.broadcasted_iota(jnp.int32, (rows, LANES), 1)
-    line[...] = jnp.zeros_like(line)
     for j in range(4):
         turned = j % 2
         offset = quarter * (j + 1) - (width - 1) if turned else quarter * j
@@ -308,6 +315,7 @@
 
 
 def place_kernel(points_ref, quarters_ref, out_ref, line):
+    line[...] = jnp.zeros_like(line)
     place(quarters_ref.at[0], points_ref[pl.program_id(0)], line)
     front = front_lanes(quarters_ref.shape[2])
     out_ref[0] = line[:, front : front + out_ref.shape[2]]

time: 27 us -> 21.6 us (0.80)
  local copies, waits for them, and re-layouts: 5.47 us -> 0 us
    unnamed x6 -> x0, local copies, waits for them, and re-layouts: 5.47 us -> none
where the time goes in v2:
time: 21.6 us; the launch traced here: 21.4 us
  Pallas kernels  20.1 us (93%)
  between operations  1.31 us (6%)
    pallas_call x1, Pallas kernels, cycle_quarters(): pl.pallas_call(functools.partial(exchange_kernel, send_groups(blocks)), i...  18.5 us
    pallas_call x1, Pallas kernels, placed(): pl.pallas_call(place_kernel, grid=(cycles,), in_specs=[pl.BlockSpec(memor...  1.62 us

profile of v2, /device:TPU:0, one launch (start us, length us, event | category | flops | bytes accessed | tf_op | source)
XLA Modules:
  0.0 21.4 jit_solution(5207585010124290426)
XLA Ops:
  1.3 18.5 %shard_map.64.quarters_ref = bf16[1,384,1408]{2,1,0:T(8,128)(2,1)S(1)} custom-call(s32[1]{0:T(128)S(6)} %copy.7.points_ref, f32[1]{0:T(128)S(6)} %copy.8.cosine_ref, s32[1280]{0:T(1024)} %wave_hbm.1, bf16[80,32,1280]{2,1,0:T(8,128)(2,1)} %zeta_hbm.1, bf16[80,32,1280]{2,1,0:T(8,128)(2,1)} %delta_hbm.1, bf16[80,16,1280]{2,1,0:T(8,128)(2,1)} %values_hbm.1), custom_call_target="tpu_custom_call" | custom-call | tf_op jit(solution)/shard_map/pallas_call | solution.py:253
  19.8 1.6 %shard_map.65 = bf16[1,96,5136]{2,1,0:T(8,128)(2,1)} custom-call(s32[1]{0:T(128)S(6)} %copy.7.points_ref, bf16[1,384,1408]{2,1,0:T(8,128)(2,1)S(1)} %shard_map.64.quarters_ref), custom_call_target="tpu_custom_call" | custom-call | tf_op jit(solution)/shard_map/pallas_call | solution.py:328

commit v3 on v2

v3 whole, which is shorter than its diff:
```python
import functools

import jax
import jax.numpy as jnp
from jax import lax
from jax.experimental import pallas as pl
from jax.experimental.pallas import tpu as pltpu
from jax.sharding import PartitionSpec as P

NLON = 5136
LANES = 128
COS = (1.0, -1 / 2, 1 / 24, -1 / 720, 1 / 40320, -1 / 3628800, 1 / 479001600,
       -1 / 87178291200, 1 / 20922789888000, -1 / 6402373705728000)
SIN = (1.0, -1 / 6, 1 / 120, -1 / 5040, 1 / 362880, -1 / 39916800, 1 / 6227020800,
       -1 / 1307674368000, 1 / 355687428096000, -1 / 121645100408832000)


def slot_block(slots):
    return max(b for b in range(1, 17) if slots % b == 0)


def degree_coefs(wave, count):
    column = lax.broadcasted_iota(jnp.int32, (wave.shape[0], count), 1)
    degree = wave + column
    living = degree < count
    positive = living & (degree > 0)
    m = wave.astype(jnp.float32)
    n = degree.astype(jnp.float32)
    radius = count / 4.0
    square = n * n
    ratio = jnp.maximum(square - m * m, 0.0) / jnp.maximum(square * (4.0 * square - 1.0), 1.0)
    lower = radius * jnp.sqrt(ratio)
    upper = pltpu.roll(lower, count - 1, 1)
    along = jnp.where(positive, -radius * m / jnp.maximum(n * (n + 1.0), 1.0), 0.0)
    before = jnp.where(positive, -lower, 0.0)
    after = jnp.where((degree > 0) & (degree + 1 < count), upper, 0.0)
    return living.astype(jnp.float32), along, before, after


def slot_fourier(values, live, along, before, after, zd):
    count = values.shape[-1]
    p = values.astype(jnp.float32)
    lon = p * along
    up, down = pltpu.roll(values, 1, 1), pltpu.roll(values, count - 1, 1)
    lat = up.astype(jnp.float32) * before + down.astype(jnp.float32) * after
    left = jnp.concatenate([p * live, lon, lat], axis=0).astype(jnp.bfloat16)
    sums = lax.dot_general(left, zd, (((1,), (1,)), ((), ())), preferred_element_type=jnp.float32)
    rows = p.shape[0]
    lev = zd.shape[0] // 4
    plain, a, b = sums[:rows], sums[rows : 2 * rows], sums[2 * rows :]
    zr, zi, dr, di = (slice(g * lev, (g + 1) * lev) for g in range(4))
    turned = jnp.concatenate([-a[:, di], a[:, dr], -a[:, zi], a[:, zr]], axis=1)
    lane = lax.broadcasted_iota(jnp.int32, b.shape, 1)
    winds = turned + jnp.where(lane < 2 * lev, -b, b)
    return jnp.concatenate([winds, plain], axis=1)


def horner(coefs, x):
    total = jnp.full_like(x, coefs[-1])
    for c in coefs[-2::-1]:
        total = total * x + c
    return total


def turn(steps, points, per_point):
    turns = jnp.round(steps * per_point)
    theta = (steps - turns * points) * (per_point * (2.0 * jnp.pi))
    square = theta * theta
    return horner(COS, square), theta * horner(SIN, square)


def columns_of(row):
    return jnp.broadcast_to(row, (LANES, row.shape[1])).T


def fill_basis(wave_col, wave_row, points, basis):
    steps = turn(wave_row * float(LANES), points, 1.0 / points)
    step_c, step_s = (columns_of(x) for x in steps)
    slots = wave_col.shape[0]
    lane = lax.broadcasted_iota(jnp.int32, (16, LANES), 1).astype(jnp.float32)
    for start in range(0, slots, 16):
        rows = slice(start, start + 16)
        c, s = turn(wave_col[rows] * lane, points, 1.0 / points)
        cs, ss = step_c[rows], step_s[rows]
        for t in range(basis.shape[1] // LANES):
            at = slice(t * LANES, (t + 1) * LANES)
            basis[rows, at] = c.astype(basis.dtype)
            basis[slots + start : slots + start + 16, at] = s.astype(basis.dtype)
            c, s = c * cs - s * ss, s * cs + c * ss


def fill_fields(arrived, m, points, cosine_sq, count, packed, at):
    x = arrived.astype(jnp.float32).T
    lev = x.shape[0] // 8
    ur, ui, vr, vi, zr, zi, dr, di = (x[g * lev : (g + 1) * lev] for g in range(8))
    q = m * (4.0 / count)
    over = 1.0 / cosine_sq
    ulr, uli, vlr, vli = -q * ui, q * ur, -q * vi, q * vr
    fields = (
        (ur, ui), (vr, vi), (ulr, uli), (vlr, vli),
        (vlr * over - zr, vli * over - zi), (dr - ulr * over, di - uli * over),
    )
    weight = jnp.where(2.0 * m < points, jnp.where(m == 0.0, 1.0, 2.0), 0.0)
    parity = jnp.where((m.astype(jnp.int32) & 1) == 0, 1.0, -1.0)
    half = len(fields) * lev
    for f, (re, im) in enumerate(fields):
        for part, x in enumerate((re * weight, -im * weight)):
            packed[part, f * lev : (f + 1) * lev, at] = x.astype(packed.dtype)
            packed[part, half + f * lev : half + (f + 1) * lev, at] = (x * parity).astype(packed.dtype)


def in_halves(devices, blocks, sb):
    return devices % 2 == 0 and blocks > 1 and sb % 16 == 0


def partners(me, devices):
    if devices % 2:
        return [lax.rem(me + off, devices) for off in range(1, devices)], []
    half = devices // 2
    side = me // half
    far = [(1 - side) * half + lax.rem(me + off, half) for off in range(half)]
    near = [side * half + lax.rem(me + off, half) for off in range(1, half)]
    return far, near


def chunks_of(me, devices, blocks, sb):
    if not in_halves(devices, blocks, sb):
        return [(devices, 0, (0, blocks), 0, devices - 1)]
    half = devices // 2
    side = me // half
    other = 1 - side
    return [
        (half, side * half, (0, blocks), 0, half - 1),
        (half, other * half, (0, blocks - 1), 1, half),
        (half, other * half, (blocks - 1, blocks), 2, half),
    ]


def exchange_kernel(
    points_ref, cosine_ref, wave_hbm, zeta_hbm, delta_hbm, values_hbm, quarters_ref,
    wave_ref, wave_col, wave_order, zeta_ref, delta_ref, values_ref, sums, sent, held, basis, packed, total,
    wave_sem, in_sem, send_sem, recv_sem,
):
    cycles, devices, blocks, sb, columns = held.shape
    count = zeta_ref.shape[-1]
    rows = values_ref.shape[1]
    own = blocks * sb
    me = lax.axis_index("wave")
    barrier = pltpu.get_barrier_semaphore()
    far, near = partners(me, devices)
    halves = in_halves(devices, blocks, sb)
    pieces = 2 if sb % 2 == 0 else 1
    piece = sb // pieces

    def fetch(step, part):
        at = pl.ds(step * sb + part * piece, piece)
        return [
            pltpu.make_async_copy(source.at[at], target.at[at], in_sem.at[k, step, part])
            for k, (source, target) in enumerate(
                ((zeta_hbm, zeta_ref), (delta_hbm, delta_ref), (values_hbm, values_ref))
            )
        ]

    def start(step, part):
        for copy in fetch(step, part):
            copy.start()

    def start_step(step):
        for part in range(pieces):
            start(step, part)

    start(0, 0)
    load_wave = pltpu.make_async_copy(wave_hbm, wave_ref, wave_sem)
    load_wave.start()
    for to in far + near:
        pl.semaphore_signal(
            barrier, inc=1, device_id={"wave": to}, device_id_type=pl.DeviceIdType.MESH
        )
    for part in range(1, pieces):
        start(0, part)

    def send(step, last):
        for to, distant in [(to, True) for to in far] + [(to, False) for to in near]:
            slot = (2 if last else 1) if halves and distant else 0
            for cycle in range(cycles):
                pltpu.make_async_remote_copy(
                    src_ref=sent.at[to * cycles + cycle, step],
                    dst_ref=held.at[cycle, me, step],
                    send_sem=send_sem.at[cycle],
                    recv_sem=recv_sem.at[cycle, slot],
                    device_id={"wave": to},
                    device_id_type=pl.DeviceIdType.MESH,
                ).start()

    load_wave.wait()
    if blocks > 1:
        start_step(1)
    wave_col[...] = columns_of(wave_ref[...].reshape(1, -1).astype(jnp.float32))

    def coefs_of(step):
        waves = wave_col[pl.ds(me * own + step * sb, sb), 0:1].astype(jnp.int32)
        return degree_coefs(waves, count)

    def transform(step, coefs, slots):
        for s in slots:
            slot = step * sb + s
            zd = jnp.concatenate([zeta_ref[slot], delta_ref[slot]], axis=0)
            out = slot_fourier(values_ref[slot], *(c[s : s + 1] for c in coefs), zd)
            sums[pl.ds(s, rows, sb), :] = out

    def await_part(step, part):
        for copy in fetch(step, part):
            copy.wait()

    def legendre(step, first):
        if first:
            coefs = coefs_of(step)
            for part in range(pieces):
                await_part(step, part)
                if part == 0 and blocks > 2:
                    start_step(2)
                transform(step, coefs, range(part * piece, (part + 1) * piece))
        else:
            for part in range(pieces):
                await_part(step, part)
            pl.when(step + 2 < blocks)(lambda: start_step(step + 2))
            transform(step, coefs_of(step), range(sb))
        sent[:, step] = sums[...].astype(sent.dtype).reshape(rows, sb, columns)
        for cycle in range(cycles):
            mine = sums[pl.ds((me * cycles + cycle) * sb, sb), :]
            held[cycle, me, step] = mine.astype(held.dtype)

    legendre(0, True)
    pl.semaphore_wait(barrier, devices - 1)
    send(0, blocks == 1)

    def middle(step, carry):
        legendre(step, False)
        pl.when(step < blocks - 1)(lambda: send(step, False))
        pl.when(step == blocks - 1)(lambda: send(step, True))
        return carry

    lax.fori_loop(1, blocks, middle, 0)
    chunks = chunks_of(me, devices, blocks, sb)
    spans = []
    for sources, first, (low, high), _, _ in chunks:
        at = spans[-1].stop if spans else 0
        spans.append(slice(at, at + sources * (high - low) * sb))
        if high - low == blocks:
            wave_order[spans[-1]] = wave_col[pl.ds(first * own, sources * own)]
        else:
            for r in range(sources):
                size = (high - low) * sb
                wave_order[at + r * size : at + (r + 1) * size] = wave_col[
                    pl.ds((first + r) * own + low * sb, size)
                ]
    slots = wave_order.shape[0]
    wave_row = wave_order[...].T[0:1]
    for cycle in range(cycles):
        points = jnp.full((1, 1), points_ref[cycle], jnp.int32).astype(jnp.float32)
        cosine_sq = jnp.full((1, 1), cosine_ref[cycle], jnp.float32)
        fill_basis(wave_order, wave_row, points, basis)
        width = basis.shape[1]
        half = packed.shape[1] // 2
        for number, (sources, first, (low, high), slot, copies) in enumerate(chunks):
            span = spans[number]
            arriving = held.at[cycle, 0:copies, low:high]
            pltpu.make_async_copy(arriving, arriving, recv_sem.at[cycle, slot]).wait()
            arrived = held[cycle, pl.ds(first, sources), low:high].reshape(-1, columns)
            fill_fields(arrived, wave_row[:, span], points, cosine_sq, count, packed, span)
            for begin in range(0, width, 256):
                at = slice(begin, min(begin + 256, width))
                both = []
                for part in range(2):
                    x = jnp.dot(
                        packed[part, :, span],
                        basis[part * slots + span.start : part * slots + span.stop, at],
                        preferred_element_type=jnp.float32,
                    )
                    if number > 0:
                        x = total[part, :, at] + x
                    if number < len(chunks) - 1:
                        total[part, :, at] = x
                    both.append(x)
                if number == len(chunks) - 1:
                    cosine, sine = both
                    parts = (
                        cosine[:half] + sine[:half], cosine[half:] - sine[half:],
                        cosine[half:] + sine[half:], cosine[:half] - sine[:half],
                    )
                    for j, x in enumerate(parts):
                        quarters_ref[cycle, j * half : (j + 1) * half, at] = x.astype(quarters_ref.dtype)
    for cycle in range(cycles):
        others = held.at[cycle, 0 : devices - 1]
        pltpu.make_async_copy(others, others, send_sem.at[cycle]).wait()


def basis_width():
    return -(-(NLON // 4 + 1) // LANES) * LANES


def cycle_quarters(points, cosine_sq, wave_of_slot, vorticity, divergence, legendre):
    slots, half, count = vorticity.shape
    lines = legendre.shape[1]
    cycles = points.shape[0]
    devices = lines // cycles
    columns = 4 * half
    rows = 6 * half
    width = basis_width()
    sb = slot_block(slots)
    blocks = slots // sb
    hbm = pl.BlockSpec(memory_space=pltpu.HBM)
    return pl.pallas_call(
        exchange_kernel,
        in_specs=[pl.BlockSpec(memory_space=pltpu.SMEM)] * 2 + [hbm] * 4,
        out_specs=pl.BlockSpec(memory_space=pltpu.VMEM),
        out_shape=jax.ShapeDtypeStruct((cycles, 2 * rows, width), jnp.bfloat16),
        scratch_shapes=[
            pltpu.VMEM(wave_of_slot.shape, jnp.int32),
            pltpu.VMEM((devices * slots, LANES), jnp.float32),
            pltpu.VMEM((devices * slots, LANES), jnp.float32),
            pltpu.VMEM(vorticity.shape, vorticity.dtype),
            pltpu.VMEM(divergence.shape, divergence.dtype),
            pltpu.VMEM(legendre.shape, legendre.dtype),
            pltpu.VMEM((lines * sb, columns), jnp.float32),
            pltpu.VMEM((lines, blocks, sb, columns), jnp.bfloat16),
            pltpu.VMEM((cycles, devices, blocks, sb, columns), jnp.bfloat16),
            pltpu.VMEM((2 * devices * slots, width), jnp.bfloat16),
            pltpu.VMEM((2, rows, devices * slots), jnp.bfloat16),
            pltpu.VMEM((2, rows, width), jnp.float32),
            pltpu.SemaphoreType.DMA,
            pltpu.SemaphoreType.DMA((3, blocks, 2)),
            pltpu.SemaphoreType.DMA((cycles,)),
            pltpu.SemaphoreType.DMA((cycles, 3)),
        ],
        compiler_params=pltpu.CompilerParams(
            collective_id=0, has_side_effects=True, vmem_limit_bytes=44 << 20
        ),
    )(points, cosine_sq, *(
        pltpu.with_memory_space_constraint(x, pltpu.HBM)
        for x in (wave_of_slot, vorticity, divergence, legendre)
    ))


def place(quarters, first, points, line):
    rows = line.shape[0]
    width = quarters.shape[1]
    field = quarters.shape[0] // 4
    tiles = width // LANES
    quarter = points // 4
    lane = lax.broadcasted_iota(jnp.int32, (rows, LANES), 1)
    for j in range(4):
        turned = j % 2
        offset = quarter * (j + 1) - (width - 1) if turned else quarter * j
        offset = offset + front_lanes(width)
        base = pl.multiple_of(offset // LANES * LANES, LANES)
        shift = offset - base
        source = lane - shift if not turned else shift - 1 - lane
        source = source & (LANES - 1)
        previous = jnp.zeros((rows, LANES), jnp.float32)
        for t in range(tiles + 1):
            rolled = jnp.zeros((rows, LANES), jnp.float32)
            if t < tiles:
                u = tiles - 1 - t if turned else t
                tile = quarters[pl.ds(first + j * field, rows), u * LANES : (u + 1) * LANES]
                point = lane + u * LANES
                keep = (point > 0) & (point <= quarter) if turned else point < quarter
                tile = jnp.where(keep, tile.astype(jnp.float32), 0.0)
                rolled = jnp.take_along_axis(tile, source, axis=1)
            moved = jnp.where(lane < shift, previous, rolled).astype(line.dtype)
            at = pl.ds(pl.multiple_of(base + t * LANES, LANES), LANES)
            line[:, at] = line[:, at] + moved
            previous = rolled


def front_lanes(width):
    return width + LANES


def place_kernel(points_ref, quarters_ref, out_ref, line):
    cycle = pl.program_id(0)
    points = points_ref[cycle]
    line[...] = jnp.zeros_like(line)
    first = pl.multiple_of(pl.program_id(1) * line.shape[0], line.shape[0])
    place(quarters_ref.at[cycle], first, points, line)
    front = front_lanes(quarters_ref.shape[2])
    out_ref[0] = line[:, front : front + out_ref.shape[2]]


def row_block(rows):
    return rows


def placed(quarters, points):
    cycles, rows, width = quarters.shape
    rows = rows // 4
    step = row_block(rows)
    line = front_lanes(width) + 4 * width + 2 * LANES
    vmem = pl.BlockSpec(memory_space=pltpu.VMEM)
    return pl.pallas_call(
        place_kernel,
        grid=(cycles, rows // step),
        in_specs=[pl.BlockSpec(memory_space=pltpu.SMEM), vmem],
        out_specs=pl.BlockSpec((1, step, NLON), lambda i, k: (i, k, 0)),
        out_shape=jax.ShapeDtypeStruct((cycles, rows, NLON), jnp.bfloat16),
        scratch_shapes=[pltpu.VMEM((step, line), jnp.bfloat16)],
        compiler_params=pltpu.CompilerParams(vmem_limit_bytes=16 << 20),
    )(points, quarters)


def body(vorticity, divergence, legendre, wave_of_slot, cycle_points, cos_squared):
    quarters = cycle_quarters(
        cycle_points, cos_squared, wave_of_slot, vorticity, divergence, legendre
    )
    return placed(quarters, cycle_points)


def solution(mesh):
    return jax.shard_map(
        body,
        mesh=mesh,
        in_specs=(
            P(("member", "wave"), None, None),
            P(("member", "wave"), None, None),
            P("wave", None, None),
            P(),
            P("wave"),
            P("wave"),
        ),
        out_specs=P(("member", "wave"), None, None),
        check_vma=False,
    )
```

time: 21.6 us -> 20 us (0.926)
  Pallas kernels: 20.1 us -> 18.6 us
    pallas_call x2, Pallas kernels: 20.1 us -> 18.6 us  [the longest x1 17 us: cycle_quarters(): pl.pallas_call(exchange_kernel, in_specs=[pl.BlockSpec(memory_space=pltpu...]
where the time goes in v3:
time: 20 us; the launch traced here: 19.9 us
  Pallas kernels  18.6 us (93%)
  between operations  1.31 us (7%)
    pallas_call x1, Pallas kernels, cycle_quarters(): pl.pallas_call(exchange_kernel, in_specs=[pl.BlockSpec(memory_space=pltpu...  17 us
    pallas_call x1, Pallas kernels, placed(): pl.pallas_call(place_kernel, grid=(cycles, rows // step), in_specs=[pl.Bl...  1.62 us

profile of v3, /device:TPU:0, one launch (start us, length us, event | category | flops | bytes accessed | tf_op | source)
XLA Modules:
  0.0 19.9 jit_solution(4362476595741510587)
XLA Ops:
  1.3 17.0 %shard_map.64.quarters_ref = bf16[1,384,1408]{2,1,0:T(8,128)(2,1)S(1)} custom-call(s32[1]{0:T(128)S(6)} %copy.7.points_ref, f32[1]{0:T(128)S(6)} %copy.8.cosine_ref, s32[1280]{0:T(1024)} %wave_hbm.1, bf16[80,32,1280]{2,1,0:T(8,128)(2,1)} %zeta_hbm.1, bf16[80,32,1280]{2,1,0:T(8,128)(2,1)} %delta_hbm.1, bf16[80,16,1280]{2,1,0:T(8,128)(2,1)} %values_hbm.1), custom_call_target="tpu_custom_call" | custom-call | tf_op jit(solution)/shard_map/pallas_call | solution.py:313
  18.3 1.6 %shard_map.65 = bf16[1,96,5136]{2,1,0:T(8,128)(2,1)} custom-call(s32[1]{0:T(128)S(6)} %copy.7.points_ref, bf16[1,384,1408]{2,1,0:T(8,128)(2,1)S(1)} %shard_map.64.quarters_ref), custom_call_target="tpu_custom_call" | custom-call | tf_op jit(solution)/shard_map/pallas_call | solution.py:400

commit v4 on v3

--- a/solution.py
+++ b/solution.py
@@ -118,7 +118,11 @@
         return [lax.rem(me + off, devices) for off in range(1, devices)], []
     half = devices // 2
     side = me // half
-    far = [(1 - side) * half + lax.rem(me + off, half) for off in range(half)]
+    run = half // 2 if half % 2 == 0 else half
+    far = []
+    for turn_of in range(half // run):
+        base = side * (turn_of * run) + (1 - side) * (devices - (turn_of + 1) * run)
+        far += [base + lax.rem(me + off, run) for off in range(run)]
     near = [side * half + lax.rem(me + off, half) for off in range(1, half)]
     return far, near
 

time: 20 us -> 20 us (level)
  no operation moved by 1% of the time
where the time goes in v4:
time: 20 us; the launch traced here: 19.8 us
  Pallas kernels  18.5 us (92%)
  between operations  1.31 us (7%)
    pallas_call x1, Pallas kernels, cycle_quarters(): pl.pallas_call(exchange_kernel, in_specs=[pl.BlockSpec(memory_space=pltpu...  16.9 us
    pallas_call x1, Pallas kernels, placed(): pl.pallas_call(place_kernel, grid=(cycles, rows // step), in_specs=[pl.Bl...  1.62 us

profile of v4, /device:TPU:0, one launch (start us, length us, event | category | flops | bytes accessed | tf_op | source)
XLA Modules:
  0.0 19.8 jit_solution(4699854376408089816)
XLA Ops:
  1.3 16.9 %shard_map.64.quarters_ref = bf16[1,384,1408]{2,1,0:T(8,128)(2,1)S(1)} custom-call(s32[1]{0:T(128)S(6)} %copy.7.points_ref, f32[1]{0:T(128)S(6)} %copy.8.cosine_ref, s32[1280]{0:T(1024)} %wave_hbm.1, bf16[80,32,1280]{2,1,0:T(8,128)(2,1)} %zeta_hbm.1, bf16[80,32,1280]{2,1,0:T(8,128)(2,1)} %delta_hbm.1, bf16[80,16,1280]{2,1,0:T(8,128)(2,1)} %values_hbm.1), custom_call_target="tpu_custom_call" | custom-call | tf_op jit(solution)/shard_map/pallas_call | solution.py:317
  18.2 1.6 %shard_map.65 = bf16[1,96,5136]{2,1,0:T(8,128)(2,1)} custom-call(s32[1]{0:T(128)S(6)} %copy.7.points_ref, bf16[1,384,1408]{2,1,0:T(8,128)(2,1)S(1)} %shard_map.64.quarters_ref), custom_call_target="tpu_custom_call" | custom-call | tf_op jit(solution)/shard_map/pallas_call | solution.py:404

commit v5 on v4

--- a/solution.py
+++ b/solution.py
@@ -122,7 +122,7 @@
     far = []
     for turn_of in range(half // run):
         base = side * (turn_of * run) + (1 - side) * (devices - (turn_of + 1) * run)
-        far += [base + lax.rem(me + off, run) for off in range(run)]
+        far += [base + side * off + (1 - side) * (run - 1 - off) for off in range(run)]
     near = [side * half + lax.rem(me + off, half) for off in range(1, half)]
     return far, near
 

time: 20 us -> 20 us (level)
  no operation moved by 1% of the time
where the time goes in v5:
time: 20 us; the launch traced here: 19.8 us
  Pallas kernels  18.5 us (92%)
  between operations  1.31 us (7%)
    pallas_call x1, Pallas kernels, cycle_quarters(): pl.pallas_call(exchange_kernel, in_specs=[pl.BlockSpec(memory_space=pltpu...  16.9 us
    pallas_call x1, Pallas kernels, placed(): pl.pallas_call(place_kernel, grid=(cycles, rows // step), in_specs=[pl.Bl...  1.61 us

profile of v5, /device:TPU:0, one launch (start us, length us, event | category | flops | bytes accessed | tf_op | source)
XLA Modules:
  0.0 19.8 jit_solution(7567518827770582641)
XLA Ops:
  1.3 16.9 %shard_map.64.quarters_ref = bf16[1,384,1408]{2,1,0:T(8,128)(2,1)S(1)} custom-call(s32[1]{0:T(128)S(6)} %copy.7.points_ref, f32[1]{0:T(128)S(6)} %copy.8.cosine_ref, s32[1280]{0:T(1024)} %wave_hbm.1, bf16[80,32,1280]{2,1,0:T(8,128)(2,1)} %zeta_hbm.1, bf16[80,32,1280]{2,1,0:T(8,128)(2,1)} %delta_hbm.1, bf16[80,16,1280]{2,1,0:T(8,128)(2,1)} %values_hbm.1), custom_call_target="tpu_custom_call" | custom-call | tf_op jit(solution)/shard_map/pallas_call | solution.py:317
  18.2 1.6 %shard_map.65 = bf16[1,96,5136]{2,1,0:T(8,128)(2,1)} custom-call(s32[1]{0:T(128)S(6)} %copy.7.points_ref, bf16[1,384,1408]{2,1,0:T(8,128)(2,1)S(1)} %shard_map.64.quarters_ref), custom_call_target="tpu_custom_call" | custom-call | tf_op jit(solution)/shard_map/pallas_call | solution.py:404
